TPU v7x, 32 devices: a whole 2x2x4 slice. The times are simulated.
32 devices in a mesh: prow: 4 (over y, core), pcol: 8 (over z, x).
Axes of the slice: x: 2, y: 2, z: 4, core: 2. Of those that a mesh axis runs over, the one named last changes fastest.
Arguments:
- matrix_slab: float32 [2048, 2048], P('pcol', 'prow'), may hold values from -1024 to 1024
- contributions: float32 [4, 256, 64, 256], P('prow', 'pcol'), may hold values from -3 to 3
- target_column: int32 [4, 256], P('prow', 'pcol'), may hold values from 0 to 31, as said below
- target_rows: int32 [4, 256], P('prow', 'pcol'), may hold values from 0 to 1
- live_rows: int32 [4, 256], P('prow', 'pcol'), may hold values from 1 to 256
- pivot_index: int32 [1, 256], replicated, may hold values from 256 to 2047, as said below
Outputs:
- factored: float32 [2048, 2048], P('pcol', 'prow')
Inputs may be any that keep to these rules, and one draw needn't show every extreme that they name: `pivot_index`: row k lists 256 distinct rows, each (k + 1) * 256 or more. `target_column`: of the 32 blocks held by one device, at most 8 have target column blocks within the columns of one index of pcol, and exactly 8 for some index.
All inputs are finite; a program needn't handle non-finite values.
Results may differ from a plain program's by a relative error of at most 0.0001.
Values sent between devices are 32-bit elements; how exact they have to be, the bound alone decides.
A program may use at most 128 MiB of HBM per device.

v0:
```python
import jax
import jax.numpy as jnp
from jax import lax
from jax.sharding import PartitionSpec as P

SLAB = 2048
PW = 256
NB = 64
TR = 256
CB_DEV = 32


HIGHEST = lax.Precision.HIGHEST


def from_root(value, axis, source):
    kept = jnp.where(lax.axis_index(axis) == source, value, 0).astype(value.dtype)
    return lax.psum(kept, axis)


def factor_block(square):
    extent = square.shape[0]
    if extent <= 16:
        for column in range(extent - 1):
            ratios = square[column + 1 :, column] / square[column, column]
            square = square.at[column + 1 :, column].set(ratios)
            square = square.at[column + 1 :, column + 1 :].add(
                -ratios[:, None] * square[column, column + 1 :][None, :]
            )
        return square
    middle = extent // 2
    top_left = factor_block(square[:middle, :middle])
    lower_unit = jnp.tril(top_left, -1) + jnp.eye(middle, dtype=square.dtype)
    upper_part = jnp.triu(top_left)
    right_part = jax.scipy.linalg.solve_triangular(
        lower_unit, square[:middle, middle:], lower=True, unit_diagonal=True
    )
    left_part = jax.scipy.linalg.solve_triangular(
        upper_part.T, square[middle:, :middle].T, lower=True
    ).T
    schur_part = square[middle:, middle:] - jnp.dot(left_part, right_part, precision=HIGHEST)
    bottom = factor_block(schur_part)
    upper_half = jnp.concatenate([top_left, right_part], axis=1)
    lower_half = jnp.concatenate([left_part, bottom], axis=1)
    return jnp.concatenate([upper_half, lower_half], axis=0)


def split_factors(packed):
    extent = packed.shape[0]
    lower_unit = jnp.tril(packed, -1) + jnp.eye(extent, dtype=packed.dtype)
    return (lower_unit, jnp.triu(packed))


def per_device(matrix_slab, contributions, target_column, target_rows, live_rows, pivot_index):
    cols_local = matrix_slab.shape[0]
    rows_local = matrix_slab.shape[1]
    row_group = lax.axis_index("prow")
    col_group = lax.axis_index("pcol")
    tile_count = rows_local // TR
    row_masks = (jnp.arange(TR)[None, :] < live_rows[0][:, None]).astype(jnp.float32)
    flattened = (contributions[0] * row_masks[:, None, :]).reshape(CB_DEV, NB * TR)
    targets = target_column[0] * tile_count + target_rows[0]
    onehot = (targets[:, None] == jnp.arange(SLAB // NB * tile_count)[None, :]).astype(jnp.float32)
    dense_sum = jnp.dot(onehot.T, flattened, precision=HIGHEST)
    dense_sum = (
        dense_sum.reshape(SLAB // NB, tile_count, NB, TR)
        .transpose(0, 2, 1, 3)
        .reshape(SLAB, rows_local)
    )
    received = lax.psum_scatter(dense_sum, "pcol", scatter_dimension=0, tiled=True)
    matrix = matrix_slab + received
    global_rows = row_group * rows_local + jnp.arange(rows_local)
    global_cols = col_group * cols_local + jnp.arange(cols_local)
    panel_end = PW
    chosen = pivot_index[0]
    pick_rows = (chosen[:, None] == global_rows[None, :]).astype(jnp.float32)
    incoming = lax.psum(jnp.dot(matrix, pick_rows.T, precision=HIGHEST), "prow")
    displaced = from_root(matrix[:, 0:panel_end], "prow", 0)
    swapped = jnp.sum(pick_rows, axis=0) > 0
    matrix = jnp.where(swapped[None, :], jnp.dot(displaced, pick_rows, precision=HIGHEST), matrix)
    matrix = matrix.at[:, 0:panel_end].set(
        jnp.where(row_group == 0, incoming, matrix[:, 0:panel_end])
    )
    select_cols = (global_cols[None, :] == 0 + jnp.arange(PW)[:, None]).astype(jnp.float32)
    owners = PW // cols_local
    pieces = [from_root(matrix, "pcol", 0 // cols_local + offset) for offset in range(owners)]
    panel_cols = jnp.concatenate(pieces, axis=0)
    diagonal = from_root(panel_cols[:, 0:panel_end], "prow", 0)
    packed = factor_block(diagonal.T)
    lower_unit, upper_part = split_factors(packed)
    lower_cols = jax.scipy.linalg.solve_triangular(upper_part.T, panel_cols, lower=True)
    upper_local = jax.scipy.linalg.solve_triangular(
        lower_unit, matrix[:, 0:panel_end].T, lower=True, unit_diagonal=True
    )
    upper_rows = from_root(upper_local, "prow", 0)
    diag_rows = (global_rows >= 0) & (global_rows < panel_end)
    below_rows = global_rows >= panel_end
    renewed = jnp.where(
        diag_rows[None, :],
        panel_cols.at[:, 0:panel_end].set(packed.T),
        jnp.where(below_rows[None, :], lower_cols, panel_cols),
    )
    placed = jnp.dot(select_cols.T, renewed, precision=HIGHEST)
    update = jnp.dot(upper_rows.T, lower_cols, precision=HIGHEST)
    filled = matrix.at[:, 0:panel_end].set(upper_rows.T)
    trailing = jnp.where(
        diag_rows[None, :], filled, jnp.where(below_rows[None, :], matrix - update, matrix)
    )
    in_panel = (global_cols >= 0) & (global_cols < panel_end)
    beyond_panel = global_cols >= panel_end
    matrix = jnp.where(
        in_panel[:, None], placed, jnp.where(beyond_panel[:, None], trailing, matrix)
    )
    return matrix


def solution(mesh):
    placed = (
        P("pcol", "prow"),
        P("prow", "pcol", None, None),
        P("prow", "pcol"),
        P("prow", "pcol"),
        P("prow", "pcol"),
        P(),
    )
    return jax.shard_map(
        per_device, mesh=mesh, in_specs=placed, out_specs=P("pcol", "prow"), check_vma=False
    )
```

profile of v0, /device:TPU:0, one launch (start us, length us, event | category | flops | bytes accessed | tf_op | source)
XLA Modules:
  0.0 1015.4 jit_solution(1840538213802180863)
XLA Ops:
  6.5 2.8 copy.245
  9.6 1.2 copy.246
  11.5 1.9 convolution_bitcast_fusion
  13.4 3.2 copy.151
  16.6 2.4 copy.247
  19.8 90.4 %reduce-scatter.2.cloned.1.call-done = f32[256,512]{1,0:T(8,128)} async-done(((f32[2048,512]{1,0:T(8,128)}), f32[256,512]{1,0:T(8,128)}) %reduce-scatter.2.cloned.1.call-update) | async-done | bytes 524304 | tf_op jit(solution)/shard_map/reduce_scatter | solution.py:70
  110.2 1.1 add.2491
  111.3 1.2 fusion.4
  114.1 32.5 %all-reduce.12.cloned.1.call-done = (f32[256,256]{1,0:T(8,128)}, f32[256,256]{1,0:T(8,128)}) async-done(((f32[256,256]{1,0:T(8,128)}, f32[256,256]{1,0:T(8,128)}), (f32[256,256]{1,0:T(8,128)}, f32[256,256]{1,0:T(8,128)})) %all-reduce.12.cloned.1.call-update) | async-done | bytes 524304 | tf_op jit(solution)/shard_map/psum | solution.py:18
  146.6 1.4 convolution_select_fusion
  148.1 1.7 constant_dynamic-update-slice_fusion
  150.9 72.6 %all-reduce.6.cloned.1.call-done = f32[256,512]{1,0:T(8,128)} async-done(((f32[256,512]{1,0:T(8,128)}), f32[256,512]{1,0:T(8,128)}) %all-reduce.6.cloned.1.call-update) | async-done | bytes 524304 | tf_op jit(solution)/shard_map/psum | solution.py:18
  223.5 1.7 select_bitcast_fusion
  225.7 31.5 %all-reduce.8.cloned.1.call-done = f32[256,256]{0,1:T(8,128)} async-done(((f32[256,256]{0,1:T(8,128)}), f32[256,256]{0,1:T(8,128)}) %all-reduce.8.cloned.1.call-update) | async-done | bytes 262160 | tf_op jit(solution)/shard_map/psum | solution.py:18
  258.0 1.2 slice.13619
  259.2 1.4 negate_bitcast_fusion.223
  295.9 1.2 custom-call.61
  297.2 1.2 custom-call.60
  298.4 1.0 fusion.141
  299.4 0.9 fusion.142
  337.9 2.4 custom-call.63
  340.4 2.5 custom-call.62
  342.9 1.0 fusion.79
  343.9 0.9 fusion.80
  344.8 0.9 convolution_subtract_fusion.9
  382.2 1.2 custom-call.65
  383.8 1.2 custom-call.64
  422.5 4.9 custom-call.67
  427.5 4.9 custom-call.66
  469.7 1.2 custom-call.69
  471.3 1.2 custom-call.68
  509.9 2.4 custom-call.71
  512.7 2.4 custom-call.70
  552.4 1.2 custom-call.73
  553.9 1.2 custom-call.72
  592.9 9.8 custom-call.35
  602.9 9.8 custom-call.34
  649.8 1.2 custom-call.75
  651.4 1.2 custom-call.74
  690.0 2.4 custom-call.77
  692.8 2.4 custom-call.76
  732.5 1.2 custom-call.79
  734.1 1.2 custom-call.78
  772.7 4.9 custom-call.81
  778.0 4.9 custom-call.80
  820.1 1.2 custom-call.83
  821.6 1.2 custom-call.82
  860.4 2.4 custom-call.85
  863.2 2.4 custom-call.84
  902.7 1.2 custom-call.87
  904.3 1.2 custom-call.86
  943.0 1.0 fusion.13
  944.8 4.6 while.486
  945.7 1.3 dynamic-slice.3416
  947.9 1.3 dynamic-slice.3416
  949.3 19.7 %custom-call.37 = f32[2,128,128]{1,2,0:T(8,128)S(1)} custom-call(f32[2,128,128]{2,1,0:T(8,128)S(1)} %get-tuple-element.5822), custom_call_target="InvertDiagBlocksLowerTriangular" | custom-call | tf_op jit(solution)/shard_map/jit(_solve_triangular)/triangular_solve | solution.py:92
  971.1 4.2 while.485
  971.8 1.4 dynamic-slice.3414
  973.9 1.4 dynamic-slice.3414
  975.4 19.7 %custom-call.36 = f32[2,128,128]{1,2,0:T(8,128)S(1)} custom-call(f32[2,128,128]{2,1,0:T(8,128)S(1)} %get-tuple-element.5814), custom_call_target="InvertDiagBlocksLowerTriangular" | custom-call | tf_op jit(solution)/shard_map/jit(_solve_triangular)/triangular_solve | solution.py:91
  996.4 7.4 all-reduce.10.cloned.1.call-done
  1003.8 1.7 fusion.12
  1005.5 1.6 fusion.3
  1007.1 1.3 convolution_select_fusion.1
  (1612 shorter events, 566.4 us)
Async XLA Ops:
  6.5 103.7 %reduce-scatter.2.cloned.1.call-start = ((), (), s32[]{:S(2)}) async-start(), calls=%async_computation.1 | async-start | bytes 4718592 | tf_op jit(solution)/shard_map/reduce_scatter | solution.py:70
  6.5 2.8 copy-start.7
  10.8 0.7 copy-start.8
  10.9 0.7 copy-start.9
  19.0 0.7 copy-start.6
  19.0 91.2 %copy-start.4 = (f32[256,512]{1,0:T(8,128)S(1)}, f32[256,512]{1,0:T(8,128)}, u32[]{:S(2)}) copy-start(f32[256,512]{1,0:T(8,128)} %param.984) | copy-start | bytes 1572868
  19.0 127.6 %all-reduce.12.cloned.1.call-start = ((), (), s32[]{:S(2)}) async-start(), calls=%async_computation.5 | async-start | bytes 1048576 | tf_op jit(solution)/shard_map/psum | solution.py:18
  113.3 110.2 %all-reduce.6.cloned.1.call-start = ((), (), s32[]{:S(2)}) async-start(), calls=%async_computation.2 | async-start | bytes 1048576 | tf_op jit(solution)/shard_map/psum | solution.py:18
  150.7 106.5 %all-reduce.8.cloned.1.call-start = ((), (), s32[]{:S(2)}) async-start(), calls=%async_computation.3 | async-start | bytes 524288 | tf_op jit(solution)/shard_map/psum | solution.py:18
  225.2 778.6 %all-reduce.10.cloned.1.call-start = ((), (), s32[]{:S(2)}) async-start(), calls=%async_computation.4 | async-start | bytes 524288 | tf_op jit(solution)/shard_map/psum | solution.py:18
  257.2 175.2 %copy-start.5 = (f32[256,256]{0,1:T(8,128)S(1)}, f32[256,256]{0,1:T(8,128)}, u32[]{:S(2)}) copy-start(f32[256,256]{0,1:T(8,128)} %all-reduce.8.cloned.1.call-done) | copy-start | bytes 786436
  768.6 174.4 %copy-start.3 = (f32[256,512]{1,0:T(8,128)S(1)}, f32[256,512]{1,0:T(8,128)}, u32[]{:S(2)}) copy-start(f32[256,512]{1,0:T(8,128)} %all-reduce.6.cloned.1.call-done) | copy-start | bytes 1572868
  944.0 0.8 copy-start.1
  969.8 25.2 %copy-start = (f32[256,512]{1,0:T(8,128)S(1)}, f32[256,512]{1,0:T(8,128)}, u32[]{:S(2)}) copy-start(f32[256,512]{1,0:T(8,128)} %all-reduce.6.cloned.1.call-done) | copy-start | bytes 1572868
  995.5 11.6 %copy-start.2 = (f32[256,512]{1,0:T(8,128)S(1)}, f32[256,512]{1,0:T(8,128)}, u32[]{:S(2)}) copy-start(f32[256,512]{1,0:T(8,128)} %copy-done.1) | copy-start | bytes 1572868
Sparse Core Ops, SparseCore 0:
  19.2 91.0 reduce-scatter.1
  113.4 33.1 all-reduce.11
  150.8 72.6 all-reduce.5
  225.7 31.4 all-reduce.7
  971.1 32.6 all-reduce.9
where the time goes:
time: 1030 us; the launch traced here: 1020 us
  local copies, waits for them, and re-layouts  388 us (38%)
  other arithmetic  308 us (30%)
  waiting for transfers between devices  235 us (23%)
  between operations  59.4 us (6%)
  matrix products  24.7 us (2%)
    mul x224, other arithmetic, factor_block(): -ratios[:, None] * square[column, column + 1:][None, :]  161 us
    psum x4, waiting for transfers between devices, from_root(): return lax.psum(kept, axis)  144 us
    scatter-add x240, local copies, waits for them, and re-layouts, factor_block(): square.at[column + 1:, column + 1:]  130 us
    slice x240, local copies, waits for them, and re-layouts, factor_block(): ratios = square[column + 1:, column] / square[column, column]  127 us
    reduce_scatter x1, waiting for transfers between devices, per_device(): lax.psum_scatter(dense_sum, 'pcol', scatter_dimension=0, tiled=True)  90.4 us
    scatter x240, local copies, waits for them, and re-layouts, factor_block(): square = square.at[column + 1:, column].set(ratios)  56.5 us
    slice x240, local copies, waits for them, and re-layouts, factor_block(): square[column, column + 1:][None, :]  50.3 us
    another operation x34, other arithmetic, factor_block(): jax.scipy.linalg.solve_triangular(lower_unit, square[:middle, middle:], l...  39.9 us
  transfers between devices with their start and end apart: 5, of which 5 were waited for; matrix products, arithmetic and copies ran while one was open for 3% of the time, Pallas kernels for 0%

commit v1 on v0

v1 whole, which is shorter than its diff:
```python
import functools

import jax
import jax.numpy as jnp
from jax import lax
from jax.experimental import pallas as pl
from jax.experimental.pallas import tpu as pltpu
from jax.sharding import PartitionSpec as P

PW = 256
NB = 64
TR = 256
B = 64

HIGHEST = lax.Precision.HIGHEST
VMEM = pltpu.VMEM
F32 = jnp.float32


def hdot(a, b):
    return jnp.dot(a, b, precision=HIGHEST, preferred_element_type=F32)


def spread_kernel(tc, tr, lr, place, pivots, blocks, slab, dense, diag, lead):
    cols = slab.shape[0]
    rows = slab.shape[1]
    dense[...] = jnp.zeros_like(dense)
    own = pl.multiple_of(place[1] * cols, cols)
    dense[pl.ds(own, cols), :] = slab[...]
    lane = lax.broadcasted_iota(jnp.int32, (NB, TR), 1)

    def add(index, carry):
        c = pl.multiple_of(tc[index] * NB, NB)
        r = pl.multiple_of(tr[index] * TR, TR)
        block = jnp.where(lane < lr[index], blocks[index], 0.0)
        dense[pl.ds(c, NB), pl.ds(r, TR)] += block
        return carry

    lax.fori_loop(0, blocks.shape[0], add, 0)
    row = place[0] * rows + lax.broadcasted_iota(jnp.int32, (PW, rows), 1)
    pick = (pivots[...] == row).astype(F32)
    panel = dense[0:PW, :]
    diag[...] = lax.dot_general(
        panel, pick, (((1,), (1,)), ((), ())), precision=HIGHEST, preferred_element_type=F32
    )
    lead[...] = jnp.where(place[0] == 0, panel[:, 0:PW], 0.0)


def eliminate(a):
    groups = B // 8
    eye = (
        lax.broadcasted_iota(jnp.int32, (B, B), 0) == lax.broadcasted_iota(jnp.int32, (B, B), 1)
    ).astype(F32)
    first = jnp.concatenate([a, eye], axis=1)
    second = jnp.concatenate([a.T, eye], axis=1)
    one = [first[8 * g : 8 * g + 8] for g in range(groups)]
    two = [second[8 * g : 8 * g + 8] for g in range(groups)]
    sub = lax.broadcasted_iota(jnp.int32, (8, 2 * B), 0)
    for k in range(B):
        g0, s0 = divmod(k, 8)
        below = sub > s0
        for which, held in enumerate((one, two)):
            col = jnp.broadcast_to(held[g0][:, k : k + 1], (8, 2 * B))
            scaled = jnp.broadcast_to((held[g0] / col)[s0 : s0 + 1, :], (8, 2 * B))
            for g in range(g0 + 1, groups):
                held[g] = held[g] - held[g][:, k : k + 1] * scaled
            fresh = held[g0] - jnp.where(below, col, 0.0) * scaled
            held[g0] = jnp.where(sub == s0, scaled, fresh) if which == 0 else fresh
    first = jnp.concatenate(one, axis=0)
    second = jnp.concatenate(two, axis=0)
    return second[:, :B].T, first[:, :B], first[:, B:], second[:, B:].T


def factor_kernel(source, packed, low_inv, up_inv):
    packed[...] = source[...]
    i = lax.broadcasted_iota(jnp.int32, (B, B), 0)
    j = lax.broadcasted_iota(jnp.int32, (B, B), 1)
    for s in range(0, PW, B):
        e = s + B
        low, up, li, ui = eliminate(packed[s:e, s:e])
        li = jnp.where(i >= j, li, 0.0)
        ui = jnp.where(i <= j, ui, 0.0)
        packed[s:e, s:e] = jnp.where(i >= j, low, up)
        low_inv[s:e, :] = li
        up_inv[s:e, :] = ui
        if e < PW:
            right = hdot(li, packed[s:e, e:])
            left = hdot(packed[e:, s:e], ui)
            packed[s:e, e:] = right
            packed[e:, s:e] = left
            packed[e:, e:] = packed[e:, e:] - hdot(left, right)


def finish_kernel(
    place, pivots, packed, low_inv, up_inv, panel, lead, diag, matrix, incoming, moved, out, x, y
):
    cols, rows = matrix.shape
    row = place[0] * rows + lax.broadcasted_iota(jnp.int32, (PW, rows), 1)
    pick = (pivots[...] == row).astype(F32)
    hit = jnp.sum(pick, axis=0, keepdims=True) > 0.0
    head = place[0] == 0
    x[...] = jnp.where(hit, hdot(lead[...], pick), panel[...])
    x[:, 0:PW] = jnp.where(head, diag[...], x[:, 0:PW])
    for s in range(0, PW, B):
        e = s + B
        part = x[s:e, :]
        if s:
            part = part - hdot(packed[s:e, 0:s], x[0:s, :])
        x[s:e, :] = hdot(low_inv[s:e, :], part)
        part = incoming[:, s:e]
        if s:
            part = part - hdot(y[:, 0:s], packed[0:s, s:e])
        y[:, s:e] = hdot(part, up_inv[s:e, :])
    owners = PW // cols

    @pl.when(place[1] >= owners)
    def _():
        swapped = jnp.where(hit, hdot(moved[...], pick), matrix[...])
        out[...] = swapped - hdot(y[...], x[...])
        out[:, 0:PW] = jnp.where(head, y[...], out[:, 0:PW])

    @pl.when(place[1] < owners)
    def _():
        x[:, 0:PW] = jnp.where(head, packed[...], x[:, 0:PW])
        off = pl.multiple_of(lax.rem(place[1], owners) * cols, cols)
        out[...] = x[pl.ds(off, cols), :]


def shape(*dims):
    return jax.ShapeDtypeStruct(dims, F32)


SMEM_SPEC = pl.BlockSpec(memory_space=pltpu.SMEM)
VMEM_SPEC = pl.BlockSpec(memory_space=pltpu.VMEM)
PARAMS = pltpu.CompilerParams(vmem_limit_bytes=48 * 1024 * 1024)


def per_device(slab_cols, matrix_slab, contributions, target_column, target_rows, live_rows, pivot_index):
    cols, rows = matrix_slab.shape
    row_group = lax.axis_index("prow")
    col_group = lax.axis_index("pcol")
    place = jnp.stack([row_group, col_group]).astype(jnp.int32)
    pivots = pivot_index[0][:, None]
    dense, diag_part, lead_part = pl.pallas_call(
        spread_kernel,
        out_shape=(shape(slab_cols, rows), shape(PW, PW), shape(PW, PW)),
        in_specs=[SMEM_SPEC] * 4 + [VMEM_SPEC] * 3,
        out_specs=(VMEM_SPEC,) * 3,
        compiler_params=PARAMS,
    )(target_column[0], target_rows[0], live_rows[0], place, pivots, contributions[0], matrix_slab)
    diag = lax.psum(diag_part, ("prow", "pcol"))
    packed, low_inv, up_inv = pl.pallas_call(
        factor_kernel,
        out_shape=(shape(PW, PW), shape(PW, B), shape(PW, B)),
        in_specs=[VMEM_SPEC],
        out_specs=(VMEM_SPEC,) * 3,
        compiler_params=PARAMS,
        cost_estimate=pl.CostEstimate(flops=10**10, bytes_accessed=10**7, transcendentals=0),
    )(diag)
    matrix = lax.psum_scatter(dense, "pcol", scatter_dimension=0, tiled=True)
    panel = lax.psum(dense[0:PW], "pcol")
    lead = lax.psum(lead_part, ("prow", "pcol"))
    global_rows = row_group * rows + jnp.arange(rows)
    pick = (pivots == global_rows[None, :]).astype(F32)
    mine = jnp.concatenate(
        [
            jnp.dot(matrix, pick.T, precision=HIGHEST),
            jnp.where(row_group == 0, matrix[:, 0:PW], 0.0),
        ],
        axis=0,
    )
    both = lax.psum(mine, "prow")
    return pl.pallas_call(
        finish_kernel,
        out_shape=shape(cols, rows),
        in_specs=[SMEM_SPEC] + [VMEM_SPEC] * 10,
        out_specs=VMEM_SPEC,
        scratch_shapes=[VMEM((PW, rows), F32), VMEM((cols, PW), F32)],
        compiler_params=PARAMS,
    )(place, pivots, packed, low_inv, up_inv, panel, lead, diag, matrix, both[:cols], both[cols:])


def solution(mesh):
    placed = (
        P("pcol", "prow"),
        P("prow", "pcol", None, None),
        P("prow", "pcol"),
        P("prow", "pcol"),
        P("prow", "pcol"),
        P(),
    )

    def whole(matrix_slab, *rest):
        return jax.shard_map(
            functools.partial(per_device, matrix_slab.shape[0]),
            mesh=mesh,
            in_specs=placed,
            out_specs=P("pcol", "prow"),
            check_vma=False,
        )(matrix_slab, *rest)

    return whole
```

time: 1030 us -> 305 us (0.30); the launches traced: 1020 us -> 304 us
  local copies, waits for them, and re-layouts: 388 us -> 10.4 us
  other arithmetic: 308 us -> 1.92 us
  between operations: 59.4 us -> 15.1 us
  Pallas kernels: 0 us -> 32.4 us
  matrix products: 24.7 us -> 1.55 us
    slice x488 -> x2, local copies, waits for them, and re-layouts: 178 us -> 2.93 us  [the longest x1 1.87 us: per_device(): panel = lax.psum(dense[0:PW], 'pcol')]
    mul x225 -> x0, other arithmetic: 161 us -> none  [the longest x224 161 us: factor_block(): -ratios[:, None] * square[column, column + 1:][None, :]]
    scatter-add x240 -> x0, local copies, waits for them, and re-layouts: 130 us -> none  [factor_block(): square.at[column + 1:, column + 1:]]
    another operation x70 -> x1, other arithmetic: 120 us -> 0.08 us  [per_device(): place = jnp.stack([row_group, col_group]).astype(jnp.int32)]
    scatter x240 -> x0, local copies, waits for them, and re-layouts: 56.5 us -> none  [factor_block(): square = square.at[column + 1:, column].set(ratios)]
    pallas_call x0 -> x3, Pallas kernels: none -> 32.4 us  [the longest x1 24 us: per_device(): pl.pallas_call(factor_kernel, out_shape=(shape(PW, PW), shape(PW, B), sha...]
    add x229 -> x1, other arithmetic: 18.2 us -> 0.01 us  [per_device(): global_rows = row_group * rows + jnp.arange(rows)]
    another operation x36 -> x0, matrix products: 12.7 us -> none  [the longest x15 5.75 us: factor_block(): jax.scipy.linalg.solve_triangular(upper_part.T, square[middle:, :middle]....]
  transfers between devices with their start and end apart: 5 -> 4, of which waited for: 5 -> 4; matrix products, arithmetic and copies ran while one was open for 3% -> 2% of each run, Pallas kernels for 0% -> 8%
where the time goes in v1:
time: 305 us; the launch traced here: 304 us
  waiting for transfers between devices  243 us (80%)
  Pallas kernels  32.4 us (11%)
  between operations  15.1 us (5%)
  local copies, waits for them, and re-layouts  10.4 us (3%)
    reduce_scatter x1, waiting for transfers between devices, per_device(): matrix = lax.psum_scatter(dense, 'pcol', scatter_dimension=0, tiled=True)  92.8 us
    psum x1, waiting for transfers between devices, per_device(): panel = lax.psum(dense[0:PW], 'pcol')  74.6 us
    psum x1, waiting for transfers between devices, per_device(): diag = lax.psum(diag_part, ('prow', 'pcol'))  62.3 us
    pallas_call x1, Pallas kernels, per_device(): pl.pallas_call(factor_kernel, out_shape=(shape(PW, PW), shape(PW, B), sha...  24 us
    psum x1, waiting for transfers between devices, per_device(): both = lax.psum(mine, 'prow')  12.6 us
    unnamed x22, local copies, waits for them, and re-layouts  6.6 us
  transfers between devices with their start and end apart: 4, of which 4 were waited for; matrix products, arithmetic and copies ran while one was open for 2% of the time, Pallas kernels for 8%

profile of v1, /device:TPU:0, one launch (start us, length us, event | category | flops | bytes accessed | tf_op | source)
XLA Modules:
  0.0 304.3 jit_solution(1536057317852205296)
XLA Ops:
  7.4 0.0 copy-start.10
  7.4 0.0 reduce-scatter.2.cloned.1.call-start
  7.4 0.9 copy.8.pivots
  8.3 0.1 pad_add_fusion.place
  8.3 0.0 copy-start.1
  8.3 1.6 copy-done.1
  9.9 0.0 copy-start.2
  9.9 1.0 copy-done.2
  11.0 0.0 copy-start.7
  11.0 0.7 copy-done.7
  11.6 0.0 copy-start.8
  11.6 0.7 copy-done.8
  12.3 0.0 copy-start.9
  12.3 0.7 copy-done.9
  12.9 3.4 %shard_map.64 = (f32[2048,512]{1,0:T(8,128)}, f32[256,256]{1,0:T(8,128)}, f32[256,256]{1,0:T(8,128)}) custom-call(s32[32]{0:T(128)S(1)} %bitcast.10, s32[32]{0:T(128)S(1)} %bitcast.11, s32[32]{0:T(128)S(1)} %bitcast.12, s32[2]{0:T(128)S(1)} %pad_add_fusion.place, s32[256,1]{1,0:T(8,128)S(1)} %copy.8.pivots, f32[32,64,256]{2,1,0:T(8,128)S(1)} %bitcast.9, ...), custom_call_target="tpu_custom_call" | custom-call | tf_op jit(solution)/shard_map/pallas_call | solution.py:144
  16.3 0.0 reduce-scatter.2.cloned.1.call-update
  16.4 0.0 all-reduce.9.cloned.1.call-start
  16.4 0.5 all-reduce.9.cloned.1.call-update
  16.9 0.0 all-reduce.7.cloned.1.call-start
  17.0 92.8 %reduce-scatter.2.cloned.1.call-done.matrix = f32[256,512]{1,0:T(8,128)} async-done(((f32[2048,512]{1,0:T(8,128)}), f32[256,512]{1,0:T(8,128)}) %reduce-scatter.2.cloned.1.call-update) | async-done | bytes 524304 | tf_op jit(solution)/shard_map/reduce_scatter | solution.py:160
  109.8 0.0 copy-done.10
  109.8 1.5 fusion
  111.3 1.0 slice_select_fusion
  112.3 0.9 pad_maximum_fusion
  113.2 0.0 all-reduce.7.cloned.1.call-update
  113.2 0.0 all-reduce.5.cloned.1.call-start
  113.2 1.9 slice.12
  115.1 0.0 all-reduce.5.cloned.1.call-update
  115.1 62.3 %all-reduce.9.cloned.1.call-done = (f32[256,256]{1,0:T(8,128)}, f32[256,256]{1,0:T(8,128)}) async-done(((f32[256,256]{1,0:T(8,128)}, f32[256,256]{1,0:T(8,128)}), (f32[256,256]{1,0:T(8,128)}, f32[256,256]{1,0:T(8,128)})) %all-reduce.9.cloned.1.call-update) | async-done | bytes 524304 | tf_op jit(solution)/shard_map/psum | solution.py:151
  177.4 0.0 copy-start.4
  177.4 0.9 copy-done.4
  178.3 0.0 copy-start
  178.4 0.0 copy-start.5
  178.4 0.0 copy-start.6
  178.4 24.0 %shard_map.65 = (f32[256,256]{1,0:T(8,128)S(1)}, f32[256,64]{1,0:T(8,128)S(1)}, f32[256,64]{1,0:T(8,128)S(1)}) custom-call(f32[256,256]{1,0:T(8,128)S(1)} %copy-done.4), custom_call_target="tpu_custom_call" | custom-call | flops 10000000000 | bytes 10000000 | tf_op jit(solution)/shard_map/pallas_call | solution.py:152
  202.3 12.6 %all-reduce.7.cloned.1.call-done = f32[512,256]{1,0:T(8,128)} async-done(((f32[512,256]{1,0:T(8,128)}), f32[512,256]{1,0:T(8,128)}) %all-reduce.7.cloned.1.call-update) | async-done | bytes 524304 | tf_op jit(solution)/shard_map/psum | solution.py:172
  214.9 1.1 fusion.4
  216.0 74.6 %all-reduce.5.cloned.1.call-done.panel = f32[256,512]{1,0:T(8,128)} async-done(((f32[256,512]{1,0:T(8,128)}), f32[256,512]{1,0:T(8,128)}) %all-reduce.5.cloned.1.call-update) | async-done | bytes 524304 | tf_op jit(solution)/shard_map/psum | solution.py:161
  290.6 0.0 copy-done
  290.6 0.0 copy-done.5
  290.6 0.0 copy-done.6
  290.6 0.0 copy-start.3
  290.6 1.0 copy-done.3
  291.7 5.1 %shard_map.66 = f32[256,512]{1,0:T(8,128)} custom-call(s32[2]{0:T(128)S(1)} %pad_add_fusion.place, s32[256,1]{1,0:T(8,128)S(1)} %copy.8.pivots, f32[256,256]{1,0:T(8,128)S(1)} %get-tuple-element.12.packed, f32[256,64]{1,0:T(8,128)S(1)} %get-tuple-element.13.low_inv, f32[256,64]{1,0:T(8,128)S(1)} %get-tuple-element.14.up_inv, f32[256,512]{1,0:T(8,128)S(1)} %copy-done.3, ...), custom_call_target="tpu_custom_call" | custom-call | tf_op jit(solution)/shard_map/pallas_call | solution.py:173
  (1 shorter events, 0.0 us)
Async XLA Ops:
  7.4 102.4 %copy-start.10 = (s32[1,256]{1,0:T(1,128)S(1)}, s32[1,256]{1,0:T(1,128)}, u32[]{:S(2)}) copy-start(s32[1,256]{1,0:T(1,128)} %param.11) | copy-start | bytes 3076
  7.4 102.4 %reduce-scatter.2.cloned.1.call-start = ((), (), s32[]{:S(2)}) async-start(), calls=%async_computation.2 | async-start | bytes 4718592 | tf_op jit(solution)/shard_map/reduce_scatter | solution.py:160
  8.3 1.6 copy-start.1
  9.9 1.0 copy-start.2
  11.0 0.7 copy-start.7
  11.6 0.7 copy-start.8
  12.3 0.7 copy-start.9
  16.4 161.0 %all-reduce.9.cloned.1.call-start = ((), (), s32[]{:S(2)}) async-start(), calls=%async_computation.4 | async-start | bytes 1048576 | tf_op jit(solution)/shard_map/psum | solution.py:151
  16.9 198.0 %all-reduce.7.cloned.1.call-start = ((), (), s32[]{:S(2)}) async-start(), calls=%async_computation.3 | async-start | bytes 1048576 | tf_op jit(solution)/shard_map/psum | solution.py:172
  113.2 177.4 %all-reduce.5.cloned.1.call-start = ((), (), s32[]{:S(2)}) async-start(), calls=%async_computation.1 | async-start | bytes 1048576 | tf_op jit(solution)/shard_map/psum | solution.py:161
  177.4 0.9 copy-start.4
  178.3 112.3 %copy-start = (f32[256,512]{1,0:T(8,128)S(1)}, f32[256,512]{1,0:T(8,128)}, u32[]{:S(2)}) copy-start(f32[256,512]{1,0:T(8,128)} %reduce-scatter.2.cloned.1.call-done.matrix) | copy-start | bytes 1572868
  178.4 112.3 %copy-start.5 = (f32[256,256]{1,0:T(8,128)S(1)}, f32[256,256]{1,0:T(8,128)}, u32[]{:S(2)}) copy-start(f32[256,256]{1,0:T(8,128)} %get-tuple-element.17.source.diag) | copy-start | bytes 786436
  178.4 112.3 %copy-start.6 = (f32[256,256]{1,0:T(8,128)S(1)}, f32[256,256]{1,0:T(8,128)}, u32[]{:S(2)}) copy-start(f32[256,256]{1,0:T(8,128)} %get-tuple-element.18.lead) | copy-start | bytes 786436
  290.6 1.0 copy-start.3
Sparse Core Ops, SparseCore 0:
  16.5 93.2 reduce-scatter.1
Sparse Core Ops, SparseCore 1:
  22.3 155.1 all-reduce.8
  179.6 35.3 all-reduce.6
  218.2 72.3 all-reduce.4

commit v2 on v1

--- a/solution.py
+++ b/solution.py
@@ -21,9 +21,8 @@
     return jnp.dot(a, b, precision=HIGHEST, preferred_element_type=F32)
 
 
-def spread_kernel(tc, tr, lr, place, pivots, blocks, slab, dense, diag, lead):
+def spread_kernel(tc, tr, lr, place, blocks, slab, dense):
     cols = slab.shape[0]
-    rows = slab.shape[1]
     dense[...] = jnp.zeros_like(dense)
     own = pl.multiple_of(place[1] * cols, cols)
     dense[pl.ds(own, cols), :] = slab[...]
@@ -37,13 +36,6 @@
         return carry
 
     lax.fori_loop(0, blocks.shape[0], add, 0)
-    row = place[0] * rows + lax.broadcasted_iota(jnp.int32, (PW, rows), 1)
-    pick = (pivots[...] == row).astype(F32)
-    panel = dense[0:PW, :]
-    diag[...] = lax.dot_general(
-        panel, pick, (((1,), (1,)), ((), ())), precision=HIGHEST, preferred_element_type=F32
-    )
-    lead[...] = jnp.where(place[0] == 0, panel[:, 0:PW], 0.0)
 
 
 def eliminate(a):
@@ -141,14 +133,26 @@
     col_group = lax.axis_index("pcol")
     place = jnp.stack([row_group, col_group]).astype(jnp.int32)
     pivots = pivot_index[0][:, None]
-    dense, diag_part, lead_part = pl.pallas_call(
+    dense = pl.pallas_call(
         spread_kernel,
-        out_shape=(shape(slab_cols, rows), shape(PW, PW), shape(PW, PW)),
-        in_specs=[SMEM_SPEC] * 4 + [VMEM_SPEC] * 3,
-        out_specs=(VMEM_SPEC,) * 3,
+        out_shape=shape(slab_cols, rows),
+        in_specs=[SMEM_SPEC] * 4 + [VMEM_SPEC] * 2,
+        out_specs=VMEM_SPEC,
         compiler_params=PARAMS,
-    )(target_column[0], target_rows[0], live_rows[0], place, pivots, contributions[0], matrix_slab)
-    diag = lax.psum(diag_part, ("prow", "pcol"))
+    )(target_column[0], target_rows[0], live_rows[0], place, contributions[0], matrix_slab)
+    piece = lax.psum_scatter(dense[0:PW], "pcol", scatter_dimension=0, tiled=True)
+    panel = lax.all_gather(piece, "pcol", axis=0, tiled=True)
+    global_rows = row_group * rows + jnp.arange(rows)
+    pick = (pivots == global_rows[None, :]).astype(F32)
+    leading = jnp.concatenate(
+        [
+            jnp.dot(panel, pick.T, precision=HIGHEST),
+            jnp.where(row_group == 0, panel[:, 0:PW], 0.0),
+        ],
+        axis=0,
+    )
+    leading = lax.psum(leading, "prow")
+    diag, lead = leading[:PW], leading[PW:]
     packed, low_inv, up_inv = pl.pallas_call(
         factor_kernel,
         out_shape=(shape(PW, PW), shape(PW, B), shape(PW, B)),
@@ -158,10 +162,6 @@
         cost_estimate=pl.CostEstimate(flops=10**10, bytes_accessed=10**7, transcendentals=0),
     )(diag)
     matrix = lax.psum_scatter(dense, "pcol", scatter_dimension=0, tiled=True)
-    panel = lax.psum(dense[0:PW], "pcol")
-    lead = lax.psum(lead_part, ("prow", "pcol"))
-    global_rows = row_group * rows + jnp.arange(rows)
-    pick = (pivots == global_rows[None, :]).astype(F32)
     mine = jnp.concatenate(
         [
             jnp.dot(matrix, pick.T, precision=HIGHEST),

time: 305 us -> 253 us (0.83)
  waiting for transfers between devices: 243 us -> 161 us
  blocking collectives: 0 us -> 33.5 us
    psum x3 -> x1, waiting for transfers between devices: 150 us -> 36 us  [per_device(): leading = lax.psum(leading, 'prow')]
    reduce_scatter x0 -> x1, waiting for transfers between devices: none -> 65.2 us  [per_device(): lax.psum_scatter(dense[0:PW], 'pcol', scatter_dimension=0, tiled=True)]
    reduce_scatter x1, waiting for transfers between devices: 92.8 us -> 58.6 us  [per_device(): matrix = lax.psum_scatter(dense, 'pcol', scatter_dimension=0, tiled=True)]
    all_gather x0 -> x1, blocking collectives: none -> 33.5 us  [per_device(): panel = lax.all_gather(piece, 'pcol', axis=0, tiled=True)]
    unnamed x22 -> x14, local copies, waits for them, and re-layouts: 6.6 us -> 4.6 us
  transfers between devices with their start and end apart: 4 -> 3, of which waited for: 4 -> 3; matrix products, arithmetic and copies ran while one was open for 2% -> 1% of each run, Pallas kernels for 8% -> 0%
where the time goes in v2:
time: 253 us; the launch traced here: 252 us
  waiting for transfers between devices  161 us (64%)
  blocking collectives  33.5 us (13%)
  Pallas kernels  32.3 us (13%)
  between operations  13.2 us (5%)
  local copies, waits for them, and re-layouts  7.89 us (3%)
  other arithmetic  2.75 us (1%)
    reduce_scatter x1, waiting for transfers between devices, per_device(): lax.psum_scatter(dense[0:PW], 'pcol', scatter_dimension=0, tiled=True)  65.2 us
    reduce_scatter x1, waiting for transfers between devices, per_device(): matrix = lax.psum_scatter(dense, 'pcol', scatter_dimension=0, tiled=True)  58.6 us
    psum x1, waiting for transfers between devices, per_device(): leading = lax.psum(leading, 'prow')  36 us
    all_gather x1, blocking collectives, per_device(): panel = lax.all_gather(piece, 'pcol', axis=0, tiled=True)  33.5 us
    pallas_call x1, Pallas kernels, per_device(): pl.pallas_call(factor_kernel, out_shape=(shape(PW, PW), shape(PW, B), sha...  24 us
    pallas_call x1, Pallas kernels, per_device(): pl.pallas_call(finish_kernel, out_shape=shape(cols, rows), in_specs=[SMEM...  5.07 us
  transfers between devices with their start and end apart: 3, of which 3 were waited for; matrix products, arithmetic and copies ran while one was open for 1% of the time, Pallas kernels for 0%

profile of v2, /device:TPU:0, one launch (start us, length us, event | category | flops | bytes accessed | tf_op | source)
XLA Modules:
  0.0 252.2 jit_solution(15273876987975896492)
XLA Ops:
  6.5 0.0 reduce-scatter.3.cloned.1.call-start
  6.5 0.1 pad_add_fusion.place
  6.6 0.0 copy-start.1
  6.6 1.6 copy-done.1
  8.2 0.0 copy-start.2
  8.2 1.0 copy-done.2
  9.2 0.0 copy-start.3
  9.2 0.7 copy-done.3
  9.9 0.0 copy-start.4
  9.9 0.7 copy-done.4
  10.6 0.0 copy-start.5
  10.6 0.7 copy-done.5
  11.2 3.2 %shard_map.64 = f32[2048,512]{1,0:T(8,128)} custom-call(s32[32]{0:T(128)S(1)} %bitcast.11, s32[32]{0:T(128)S(1)} %bitcast.12, s32[32]{0:T(128)S(1)} %bitcast.13, s32[2]{0:T(128)S(1)} %pad_add_fusion.place, f32[32,64,256]{2,1,0:T(8,128)S(1)} %bitcast.10, f32[256,512]{1,0:T(8,128)S(1)} %copy-done.2), custom_call_target="tpu_custom_call" | custom-call | tf_op jit(solution)/shard_map/pallas_call | solution.py:136
  14.4 0.0 copy-start.6
  14.4 1.9 slice.28
  16.3 0.0 reduce-scatter.3.cloned.1.call-update
  16.3 0.0 reduce-scatter.5.cloned.1.call-start
  16.4 0.7 reduce-scatter.5.cloned.1.call-update
  17.1 0.0 all-reduce.3.cloned.1.call-start
  17.2 65.2 %reduce-scatter.3.cloned.1.call-done = f32[32,512]{1,0:T(8,128)} async-done(((f32[256,512]{1,0:T(8,128)}), f32[32,512]{1,0:T(8,128)}) %reduce-scatter.3.cloned.1.call-update) | async-done | bytes 65552 | tf_op jit(solution)/shard_map/reduce_scatter | solution.py:143
  82.3 33.5 %all_gather.3.panel = f32[256,512]{1,0:T(8,128)S(1)} all-gather(f32[32,512]{1,0:T(8,128)} %reduce-scatter.3.cloned.1.call-done), channel_id=1, replica_groups=mesh['prow'=4,'pcol'=8] {'pcol'}, dimensions={0}, use_global_device_ids=true | all-gather | bytes 589824 | tf_op jit(solution)/shard_map/all_gather | solution.py:144
  115.9 0.0 copy-done.6
  115.9 0.5 fusion.2
  116.4 0.8 pad_maximum_fusion
  117.2 58.6 %reduce-scatter.5.cloned.1.call-done.matrix = f32[256,512]{1,0:T(8,128)} async-done(((f32[2048,512]{1,0:T(8,128)}), f32[256,512]{1,0:T(8,128)}) %reduce-scatter.5.cloned.1.call-update) | async-done | bytes 524304 | tf_op jit(solution)/shard_map/reduce_scatter | solution.py:164
  175.9 1.5 fusion
  177.4 1.0 slice_select_fusion
  178.4 0.9 pad_maximum_fusion.1
  179.2 0.0 all-reduce.3.cloned.1.call-update
  179.3 0.1 copy.7.pivots
  179.4 36.0 %all-reduce.3.cloned.1.call-done = (f32[512,256]{1,0:T(8,128)}, f32[512,256]{1,0:T(8,128)}) async-done(((f32[512,256]{1,0:T(8,128)}, f32[512,256]{1,0:T(8,128)}), (f32[512,256]{1,0:T(8,128)}, f32[512,256]{1,0:T(8,128)})) %all-reduce.3.cloned.1.call-update) | async-done | bytes 1048592 | tf_op jit(solution)/shard_map/psum | solution.py:154
  215.4 1.3 fusion.8
  216.7 0.0 copy-start
  216.7 24.0 %shard_map.65 = (f32[256,256]{1,0:T(8,128)S(1)}, f32[256,64]{1,0:T(8,128)S(1)}, f32[256,64]{1,0:T(8,128)S(1)}) custom-call(f32[256,256]{1,0:T(8,128)S(1)} %get-tuple-element.17.source.diag), custom_call_target="tpu_custom_call" | custom-call | flops 10000000000 | bytes 10000000 | tf_op jit(solution)/shard_map/pallas_call | solution.py:156
  240.6 0.0 copy-done
  240.6 5.1 %shard_map.66 = f32[256,512]{1,0:T(8,128)} custom-call(s32[2]{0:T(128)S(1)} %pad_add_fusion.place, s32[256,1]{1,0:T(8,128)S(1)} %copy.7.pivots, f32[256,256]{1,0:T(8,128)S(1)} %get-tuple-element.8.packed, f32[256,64]{1,0:T(8,128)S(1)} %get-tuple-element.9.low_inv, f32[256,64]{1,0:T(8,128)S(1)} %get-tuple-element.10.up_inv, f32[256,512]{1,0:T(8,128)S(1)} %all_gather.3.panel, ...), custom_call_target="tpu_custom_call" | custom-call | tf_op jit(solution)/shard_map/pallas_call | solution.py:173
  (2 shorter events, 0.0 us)
Async XLA Ops:
  6.5 75.8 %reduce-scatter.3.cloned.1.call-start = ((), (), s32[]{:S(2)}) async-start(), calls=%async_computation.2 | async-start | bytes 589824 | tf_op jit(solution)/shard_map/reduce_scatter | solution.py:143
  6.6 1.6 copy-start.1
  8.2 1.0 copy-start.2
  9.2 0.7 copy-start.3
  9.9 0.7 copy-start.4
  10.6 0.7 copy-start.5
  14.4 101.4 %copy-start.6 = (s32[1,256]{1,0:T(1,128)S(1)}, s32[1,256]{1,0:T(1,128)}, u32[]{:S(2)}) copy-start(s32[1,256]{1,0:T(1,128)} %param.11) | copy-start | bytes 3076
  16.3 159.5 %reduce-scatter.5.cloned.1.call-start = ((), (), s32[]{:S(2)}) async-start(), calls=%async_computation.3 | async-start | bytes 4718592 | tf_op jit(solution)/shard_map/reduce_scatter | solution.py:164
  17.1 198.3 %all-reduce.3.cloned.1.call-start = ((), (), s32[]{:S(2)}) async-start(), calls=%async_computation.4 | async-start | bytes 2097152 | tf_op jit(solution)/shard_map/psum | solution.py:154
  216.7 24.0 %copy-start = (f32[256,512]{1,0:T(8,128)S(1)}, f32[256,512]{1,0:T(8,128)}, u32[]{:S(2)}) copy-start(f32[256,512]{1,0:T(8,128)} %reduce-scatter.5.cloned.1.call-done.matrix) | copy-start | bytes 1572868
Sparse Core Ops, SparseCore 0:
  16.5 65.8 reduce-scatter.2
  86.0 89.8 reduce-scatter.4
  179.4 35.9 all-reduce.2
